TPU v7x, 32 devices: a whole 2x2x4 slice. The times are simulated.
32 devices in a mesh: lat: 16 (over z, y, x), batch: 2 (over core).
Axes of the slice: x: 2, y: 2, z: 4, core: 2. Of those that a mesh axis runs over, the one named last changes fastest.
Arguments:
- fields: bfloat16 [2, 192, 384, 384], P('batch', 'lat'), may hold values from -6 to 6
- cotangent: bfloat16 [2, 192, 384, 384], P('batch', 'lat'), may hold values from -6 to 6
- weights: bfloat16 [128, 2, 384, 384], P('lat'), may hold values from -0.21875 to 0.21875
- degree_of: int32 [128], replicated, may hold values from 0 to 127, each once
Outputs:
- grad_fields: bfloat16 [2, 192, 384, 384], P('batch', 'lat')
- grad_weights: bfloat16 [128, 2, 384, 384], P('lat')
Inputs may be any that keep to these rules, and one draw needn't show every extreme that they name: `degree_of`: each degree 0 to 127 is held by exactly one slot.
All inputs are finite; a program needn't handle non-finite values.
Results may differ from a plain program's by a relative error of at most 0.018.
Values may be sent and summed in bfloat16 or wider, within the bound.
A program may use at most 64 MiB of HBM per device.

v0:
```python
import jax
import jax.numpy as jnp
from jax import lax
from jax.sharding import PartitionSpec as P

LATS = 192
LONS = 384
ORDERS = 128
DEGREES = 128
CHANNELS = 384


def legendre_table(order_ids, lat_count, degree_count):
    colatitude = jnp.pi * (jnp.arange(lat_count, dtype=jnp.float32) + 0.5) / lat_count
    cosine = jnp.cos(colatitude)[None, :]
    log_sine = jnp.log(jnp.sin(colatitude))[None, :]
    order_col = order_ids[:, None]
    order_real = order_col.astype(jnp.float32)
    steps_up = jnp.arange(1, degree_count + 1, dtype=jnp.float32)[None, :]
    factor = jnp.where(
        steps_up <= order_real, 0.5 * jnp.log((2.0 * steps_up + 1.0) / (2.0 * steps_up)), 0.0
    )
    log_start = 0.5 * jnp.log(1.0 / (4.0 * jnp.pi)) + jnp.sum(factor, axis=1, keepdims=True)
    diagonal = jnp.exp(log_start + order_real * log_sine)
    squared = order_real * order_real

    def advance(carry, degree):
        previous, older = carry
        degree_real = degree.astype(jnp.float32)
        lead = jnp.sqrt(
            jnp.maximum(4.0 * degree_real * degree_real - 1.0, 0.0)
            / jnp.maximum(degree_real * degree_real - squared, 1.0)
        )
        lower = degree_real - 1.0
        back = jnp.sqrt(
            jnp.maximum(lower * lower - squared, 0.0) / jnp.maximum(4.0 * lower * lower - 1.0, 1.0)
        )
        general = lead * (cosine * previous - back * older)
        first = jnp.sqrt(2.0 * order_real + 3.0) * cosine * previous
        value = jnp.where(
            degree == order_col,
            diagonal,
            jnp.where(
                degree == order_col + 1, first, jnp.where(degree > order_col + 1, general, 0.0)
            ),
        )
        return ((value, previous), value)

    zeros = jnp.zeros((order_ids.shape[0], lat_count), jnp.float32)
    final_state, table = lax.scan(
        advance, (zeros, zeros), jnp.arange(degree_count, dtype=jnp.int32)
    )
    return jnp.transpose(table, (1, 0, 2))


def spectral_tables(start, ord_dev, degree_of):
    order_ids = start + jnp.arange(ord_dev, dtype=jnp.int32)
    mine = legendre_table(order_ids, LATS, DEGREES)
    selector = (degree_of[:, None] == jnp.arange(DEGREES, dtype=jnp.int32)[None, :]).astype(
        jnp.float32
    )
    chosen = jnp.einsum("mli,jl->mji", mine, selector, precision=lax.Precision.HIGHEST)
    colatitude = jnp.pi * (jnp.arange(LATS, dtype=jnp.float32) + 0.5) / LATS
    quadrature = 2.0 * jnp.pi * jnp.pi / LATS * jnp.sin(colatitude)
    return ((chosen * quadrature[None, None, :]).astype(jnp.bfloat16), chosen.astype(jnp.bfloat16))


def fourier_tables(lon_count, order_count):
    lon_ids = jnp.arange(lon_count, dtype=jnp.int32)[:, None]
    order_ids = jnp.arange(order_count, dtype=jnp.int32)[None, :]
    phase = 2.0 * jnp.pi * (lon_ids * order_ids % lon_count).astype(jnp.float32) / lon_count
    forward = (
        jnp.stack([jnp.cos(phase), -jnp.sin(phase)], axis=2).reshape(lon_count, 2 * order_count)
        / lon_count
    )
    doubled = jnp.where(order_ids == 0, 1.0, 2.0)
    inverse = jnp.stack([doubled * jnp.cos(phase), -doubled * jnp.sin(phase)], axis=2).reshape(
        lon_count, 2 * order_count
    )
    return (forward.astype(jnp.bfloat16), jnp.transpose(inverse).astype(jnp.bfloat16))


def to_orders(values):
    return lax.all_to_all(values, "lat", split_axis=1, concat_axis=0, tiled=True)


def to_degrees(values):
    return lax.all_to_all(values, "lat", split_axis=0, concat_axis=1, tiled=True)


def back_to_orders(values):
    return lax.all_to_all(values, "lat", split_axis=1, concat_axis=0, tiled=True)


def to_bands(values):
    return lax.all_to_all(values, "lat", split_axis=0, concat_axis=1, tiled=True)


def product(spec, left, right):
    return jnp.einsum(spec, left, right, preferred_element_type=jnp.float32)


def apply_filter(coeffs, weights):
    c_real = coeffs[:, :, 0]
    c_imag = coeffs[:, :, 1]
    w_real = weights[:, 0]
    w_imag = weights[:, 1]
    f_real = product("jmsc,jcd->jmsd", c_real, w_real) - product("jmsc,jcd->jmsd", c_imag, w_imag)
    f_imag = product("jmsc,jcd->jmsd", c_real, w_imag) + product("jmsc,jcd->jmsd", c_imag, w_real)
    return jnp.stack([f_real, f_imag], axis=2).astype(jnp.bfloat16)


def adjoint_filter(grads, weights):
    g_real = grads[:, :, 0]
    g_imag = grads[:, :, 1]
    w_real = weights[:, 0]
    w_imag = weights[:, 1]
    a_real = product("jmsd,jcd->jmsc", g_real, w_real) + product("jmsd,jcd->jmsc", g_imag, w_imag)
    a_imag = product("jmsd,jcd->jmsc", g_imag, w_real) - product("jmsd,jcd->jmsc", g_real, w_imag)
    return jnp.stack([a_real, a_imag], axis=2).astype(jnp.bfloat16)


def filter_grad(coeffs, grads):
    c_real = coeffs[:, :, 0]
    c_imag = coeffs[:, :, 1]
    g_real = grads[:, :, 0]
    g_imag = grads[:, :, 1]
    dw_real = product("jmsc,jmsd->jcd", c_real, g_real) + product("jmsc,jmsd->jcd", c_imag, g_imag)
    dw_imag = product("jmsc,jmsd->jcd", c_real, g_imag) - product("jmsc,jmsd->jcd", c_imag, g_real)
    return jnp.stack([dw_real, dw_imag], axis=1)


def local(fields, cotangent, weights, degree_of):
    samples = fields.shape[0]
    band_rows = fields.shape[1]
    ord_dev = ORDERS // lax.axis_size("lat")
    forward, inverse = fourier_tables(LONS, ORDERS)
    qslot, pslot = spectral_tables(lax.axis_index("lat") * ord_dev, ord_dev, degree_of)
    spectra = product("sikc,kf->ifsc", fields, forward).astype(jnp.bfloat16)
    spectra = spectra.reshape(band_rows, ORDERS, 2, samples, CHANNELS)
    gathered = to_orders(spectra)
    coeffs_local = product("mji,imrsc->jmrsc", qslot, gathered).astype(jnp.bfloat16)
    coeffs = to_degrees(coeffs_local)
    filtered = apply_filter(coeffs, weights)
    returned = back_to_orders(filtered)
    synth_local = product("mji,jmrsc->imrsc", pslot, returned).astype(jnp.bfloat16)
    synth = to_bands(synth_local)
    response = product(
        "ifsc,fk->sikc", synth.reshape(band_rows, 2 * ORDERS, samples, CHANNELS), inverse
    )
    activated, pullback = jax.vjp(jax.nn.gelu, response)
    upstream = pullback(cotangent.astype(jnp.float32))[0].astype(jnp.bfloat16)
    grad_synth = product("sikc,fk->ifsc", upstream, inverse).astype(jnp.bfloat16)
    grad_synth = grad_synth.reshape(band_rows, ORDERS, 2, samples, CHANNELS)
    grad_gathered = to_orders(grad_synth)
    grad_local = product("mji,imrsc->jmrsc", pslot, grad_gathered).astype(jnp.bfloat16)
    grad_filtered = to_degrees(grad_local)
    weight_total = lax.psum(filter_grad(coeffs, grad_filtered).astype(jnp.bfloat16), "batch")
    grad_coeffs = adjoint_filter(grad_filtered, weights)
    grad_back = back_to_orders(grad_coeffs)
    grad_local_spec = product("mji,jmrsc->imrsc", qslot, grad_back).astype(jnp.bfloat16)
    grad_bands = to_bands(grad_local_spec)
    delta = product(
        "ifsc,kf->sikc", grad_bands.reshape(band_rows, 2 * ORDERS, samples, CHANNELS), forward
    )
    grad_fields = (cotangent.astype(jnp.float32) + delta).astype(jnp.bfloat16)
    return (grad_fields, weight_total)


def solution(mesh):
    return jax.shard_map(
        local,
        mesh=mesh,
        in_specs=(
            P("batch", "lat", None, None),
            P("batch", "lat", None, None),
            P("lat", None, None, None),
            P(),
        ),
        out_specs=(P("batch", "lat", None, None), P("lat", None, None, None)),
        check_vma=False,
    )
```

profile of v0, /device:TPU:12, one launch (start us, length us, event | category | flops | bytes accessed | tf_op | source)
XLA Modules:
  0.0 810.1 jit_solution(15554122631083850034)
XLA Ops:
  7.2 0.8 fusion.118
  8.0 0.7 fusion.105
  8.7 1.8 copy.176
  10.5 1.7 reshape.493
  12.2 3.7 convert_bitcast_fusion.3
  15.9 4.8 reshape.480
  20.8 3.0 copy.178
  23.8 7.2 all-to-all-start
  31.3 351.8 %while.21 = (s32[]{:T(128)}, f32[8,192]{1,0:T(8,128)S(1)}, f32[8,192]{1,0:T(8,128)S(1)}, f32[128,8,192]{2,1,0:T(8,128)S(1)}, s32[128]{0:T(128)S(1)}, /*index=5*/...) while((s32[]{:T(128)}, f32[8,192]{1,0:T(8,128)S(1)}, ...), condition=%wide.region_2.3_spmd.clone.clone.clone.clone, body=%wide.region_1.2_spmd.clone.clone.clone.clone.sunk | while | flops 18991 | bytes 48339 | solution.py:50
  32.6 0.6 compare_bitcast_fusion.5
  35.3 0.6 compare_bitcast_fusion.5
  38.1 0.6 compare_bitcast_fusion.5
  40.8 0.6 compare_bitcast_fusion.5
  43.6 0.6 compare_bitcast_fusion.5
  46.3 0.6 compare_bitcast_fusion.5
  49.1 0.6 compare_bitcast_fusion.5
  51.8 0.6 compare_bitcast_fusion.5
  54.6 0.6 compare_bitcast_fusion.5
  384.1 2.1 copy.249
  386.6 1.4 fusion.79
  388.0 2.9 copy.183
  390.9 43.2 %all_to_all.126 = bf16[128,8,2,1,384]{4,2,1,3,0:T(2,128)(2,1)S(1)} all-to-all(bf16[128,8,2,1,384]{4,2,1,3,0:T(2,128)(2,1)} %copy.183), channel_id=1, replica_groups=mesh['lat'=16,'batch'=2] {'lat'}, dimensions={0} | all-to-all | bytes 3145728 | tf_op jit(solution)/shard_map/all_to_all | solution.py:88
  434.7 0.7 fusion.40
  435.4 0.7 fusion.38
  436.1 0.7 fusion.90
  436.8 0.7 fusion.93
  437.7 0.9 copy.188
  438.7 40.7 %all_to_all.127 = bf16[8,128,2,1,384]{4,0,3,2,1:T(8,128)(2,1)S(1)} all-to-all(bf16[8,128,2,1,384]{4,0,3,2,1:T(8,128)(2,1)S(1)} %copy.188), channel_id=1, replica_groups=mesh['lat'=16,'batch'=2] {'lat'}, dimensions={1} | all-to-all | bytes 3145728 | tf_op jit(solution)/shard_map/all_to_all | solution.py:92
  479.3 0.8 convert_bitcast_fusion.2
  480.1 3.8 copy.190
  483.9 5.9 all-to-all-start.3
  489.9 0.8 multiply_convert_fusion.1
  491.1 51.3 %all-to-all-done.3 = bf16[192,8,2,1,384]{4,2,1,3,0:T(2,128)(2,1)} async-done(((bf16[192,8,2,1,384]{4,2,1,3,0:T(2,128)(2,1)}), bf16[192,8,2,1,384]{4,2,1,3,0:T(2,128)(2,1)}, u32[]{:S(2)}, u32[]{:S(2)}) %all-to-all-start.3) | async-done | bytes 2359328 | tf_op jit(solution)/shard_map/all_to_all | solution.py:96
  542.4 2.1 copy.191
  544.5 3.8 copy.192
  548.3 6.1 reshape.485
  554.5 9.2 %convert_bitcast_fusion.1 = bf16[12,256,1,384]{3,1,0,2:T(8,128)(2,1)} fusion(bf16[384,256,1]{0,1,2:T(8,128)(2,1)S(1)} %reshape.499, bf16[1,12,384,384]{3,2,1,0:T(8,128)(2,1)} %param.7, bf16[12,256,384]{2,1,0:T(8,128)(2,1)} %reshape.485, bf16[384,256]{0,1:T(8,128)(2,1)S(1)} %convert_element_type.174), kind=kOutput, calls=%fused_computation.70 | convolution fusion | flops 1850277888 | bytes 8650752 | tf_op jit(solution)/shard_map/sikc,fk->ifsc/dot_general | solution.py:100
  563.6 5.9 reshape.487
  569.5 3.3 copy.194
  572.8 57.6 %all_to_all.128 = bf16[12,128,2,1,384]{4,2,0,3,1:T(2,128)(2,1)S(1)} all-to-all(bf16[12,128,2,1,384]{4,2,0,3,1:T(2,128)(2,1)S(1)} %copy.194), channel_id=1, replica_groups=mesh['lat'=16,'batch'=2] {'lat'}, dimensions={1} | all-to-all | bytes 4718592 | tf_op jit(solution)/shard_map/all_to_all | solution.py:84
  631.2 2.4 fusion.76
  633.7 4.9 copy.198
  638.6 41.2 %all_to_all.129 = bf16[128,8,2,1,384]{4,2,1,3,0:T(2,128)(2,1)S(1)} all-to-all(bf16[128,8,2,1,384]{4,2,1,3,0:T(2,128)(2,1)} %copy.198), channel_id=1, replica_groups=mesh['lat'=16,'batch'=2] {'lat'}, dimensions={0} | all-to-all | bytes 3145728 | tf_op jit(solution)/shard_map/all_to_all | solution.py:88
  680.3 0.9 fusion.36
  681.2 0.9 fusion.34
  682.1 0.9 fusion.96
  683.1 0.9 fusion.99
  684.2 2.1 copy.201
  686.2 5.5 all-to-all-start.6
  691.9 2.1 fusion.103
  694.0 0.8 fusion.32
  694.8 0.8 fusion.102
  695.7 0.8 fusion.33
  696.5 2.7 pad_maximum_fusion
  699.2 28.6 %all-to-all-done.6 = bf16[8,128,2,1,384]{4,0,3,2,1:T(8,128)(2,1)} async-done(((bf16[8,128,2,1,384]{4,0,3,2,1:T(8,128)(2,1)}), bf16[8,128,2,1,384]{4,0,3,2,1:T(8,128)(2,1)}, u32[]{:S(2)}, u32[]{:S(2)}) %all-to-all-start.6) | async-done | bytes 1572896 | tf_op jit(solution)/shard_map/all_to_all | solution.py:92
  727.8 2.3 convert_bitcast_fusion
  730.2 3.8 copy.203
  734.0 4.8 all-to-all-start.7
  738.9 0.8 convert_element_type.173
  739.6 5.1 copy.211
  744.8 47.2 %all-to-all-done.7 = bf16[192,8,2,1,384]{4,2,1,3,0:T(2,128)(2,1)S(1)} async-done(((bf16[192,8,2,1,384]{4,2,1,3,0:T(2,128)(2,1)}), bf16[192,8,2,1,384]{4,2,1,3,0:T(2,128)(2,1)S(1)}, u32[]{:S(2)}, u32[]{:S(2)}) %all-to-all-start.7) | async-done | bytes 2359328 | tf_op jit(solution)/shard_map/all_to_all | solution.py:96
  792.4 2.4 copy.205
  794.9 2.4 reshape.492
  797.2 5.8 fusion.24
  (941 shorter events, 264.3 us)
Async XLA Ops:
  7.2 5.0 copy-start
  23.8 360.4 %all-to-all-start = ((bf16[12,128,2,1,384]{4,2,0,3,1:T(2,128)(2,1)}), bf16[12,128,2,1,384]{4,2,0,3,1:T(2,128)(2,1)}, u32[]{:S(2)}, u32[]{:S(2)}) async-start(bf16[12,128,2,1,384]{4,2,0,3,1:T(2,128)(2,1)} %copy.178), calls=%async_computation | async-start | bytes 4718592 | tf_op jit(solution)/shard_map/all_to_all | solution.py:84
  30.9 352.6 %copy-start.5 = (s32[128]{0:T(128)S(1)}, s32[128]{0:T(128)}, u32[]{:S(2)}) copy-start(s32[128]{0:T(128)} %param.9) | copy-start | bytes 1540
  386.6 48.1 %slice-start = ((s8[4718592]{0:T(1024)(128)(4,1)}), s8[524288]{0:T(1024)(128)(4,1)S(1)}, s32[]{:S(2)}) async-start(s8[4718592]{0:T(1024)(128)(4,1)} %bitcast.253), calls=%async_computation.9 | async-start | bytes 1048576
  390.9 43.8 %slice-start.1 = ((s8[4718592]{0:T(1024)(128)(4,1)}), s8[4194304]{0:T(1024)(128)(4,1)S(1)}, s32[]{:S(2)}) async-start(s8[4718592]{0:T(1024)(128)(4,1)} %bitcast.253), calls=%async_computation.10 | async-start | bytes 8388608
  483.9 58.4 %all-to-all-start.3 = ((bf16[192,8,2,1,384]{4,2,1,3,0:T(2,128)(2,1)}), bf16[192,8,2,1,384]{4,2,1,3,0:T(2,128)(2,1)}, u32[]{:S(2)}, u32[]{:S(2)}) async-start(bf16[192,8,2,1,384]{4,2,1,3,0:T(2,128)(2,1)} %copy.190), calls=%async_computation.3 | async-start | bytes 4718592 | tf_op jit(solution)/shard_map/all_to_all | solution.py:96
  631.2 49.1 %slice-start.2 = ((s8[4718592]{0:T(1024)(128)(4,1)}), s8[524288]{0:T(1024)(128)(4,1)S(1)}, s32[]{:S(2)}) async-start(s8[4718592]{0:T(1024)(128)(4,1)} %bitcast.255), calls=%async_computation.11 | async-start | bytes 1048576
  638.6 41.7 %slice-start.3 = ((s8[4718592]{0:T(1024)(128)(4,1)}), s8[4194304]{0:T(1024)(128)(4,1)S(1)}, s32[]{:S(2)}) async-start(s8[4718592]{0:T(1024)(128)(4,1)} %bitcast.255), calls=%async_computation.12 | async-start | bytes 8388608
  680.3 2.8 copy-start.2
  686.2 41.6 %all-to-all-start.6 = ((bf16[8,128,2,1,384]{4,0,3,2,1:T(8,128)(2,1)}), bf16[8,128,2,1,384]{4,0,3,2,1:T(8,128)(2,1)}, u32[]{:S(2)}, u32[]{:S(2)}) async-start(bf16[8,128,2,1,384]{4,0,3,2,1:T(8,128)(2,1)} %copy.201), calls=%async_computation.6 | async-start | bytes 3145728 | tf_op jit(solution)/shard_map/all_to_all | solution.py:92
  691.7 47.9 %all-reduce.2.cloned.1.call-start = ((), (), s32[]{:S(2)}) async-start(), calls=%async_computation.8 | async-start | bytes 9437184 | tf_op jit(solution)/shard_map/psum | solution.py:158
  691.9 2.1 copy-start.3
  734.0 4.8 copy-start.4
  734.0 58.0 %all-to-all-start.7 = ((bf16[192,8,2,1,384]{4,2,1,3,0:T(2,128)(2,1)}), bf16[192,8,2,1,384]{4,2,1,3,0:T(2,128)(2,1)S(1)}, u32[]{:S(2)}, u32[]{:S(2)}) async-start(bf16[192,8,2,1,384]{4,2,1,3,0:T(2,128)(2,1)} %copy.203), calls=%async_computation.7 | async-start | bytes 4718592 | tf_op jit(solution)/shard_map/all_to_all | solution.py:96
  797.2 5.8 copy-start.1
Sparse Core Ops, SparseCore 0:
  699.3 30.0 all-reduce.1
where the time goes:
time: 822 us; the launch traced here: 810 us
  other arithmetic  192 us (23%)
  blocking collectives  183 us (22%)
  local copies, waits for them, and re-layouts  147 us (18%)
  waiting for transfers between devices  127 us (15%)
  loops' own time  86.7 us (11%)
  matrix products  37.1 us (5%)
  starting transfers between devices  23.6 us (3%)
  between operations  14.7 us (2%)
    all_to_all x2, waiting for transfers between devices, to_bands(): lax.all_to_all(values, 'lat', split_axis=0, concat_axis=1, tiled=True)  98.5 us
    another operation x1, loops' own time, legendre_table(): lax.scan(advance, (zeros, zeros), jnp.arange(degree_count, dtype=jnp.int32))  86.7 us
    all_to_all x2, blocking collectives, to_degrees(): lax.all_to_all(values, 'lat', split_axis=0, concat_axis=1, tiled=True)  84.4 us
    gt x128, other arithmetic, advance(): degree > order_col + 1  82.3 us
    eq x128, other arithmetic, advance(): degree == order_col  81.4 us
    dynamic_slice x128, local copies, waits for them, and re-layouts, legendre_table(): lax.scan(advance, (zeros, zeros), jnp.arange(degree_count, dtype=jnp.int32))  79.2 us
    all_to_all x1, blocking collectives, to_orders(): lax.all_to_all(values, 'lat', split_axis=1, concat_axis=0, tiled=True)  57.6 us
    all_to_all x1, blocking collectives, back_to_orders(): lax.all_to_all(values, 'lat', split_axis=1, concat_axis=0, tiled=True)  40.7 us
  transfers between devices with their start and end apart: 5, of which 3 were waited for; matrix products, arithmetic and copies ran while one was open for 35% of the time, Pallas kernels for 0%

commit v1 on v0

--- a/solution.py
+++ b/solution.py
@@ -1,6 +1,8 @@
 import jax
 import jax.numpy as jnp
 from jax import lax
+from jax.experimental import pallas as pl
+from jax.experimental.pallas import tpu as pltpu
 from jax.sharding import PartitionSpec as P
 
 LATS = 192
@@ -8,23 +10,27 @@
 ORDERS = 128
 DEGREES = 128
 CHANNELS = 384
-
-
-def legendre_table(order_ids, lat_count, degree_count):
-    colatitude = jnp.pi * (jnp.arange(lat_count, dtype=jnp.float32) + 0.5) / lat_count
-    cosine = jnp.cos(colatitude)[None, :]
-    log_sine = jnp.log(jnp.sin(colatitude))[None, :]
-    order_col = order_ids[:, None]
-    order_real = order_col.astype(jnp.float32)
-    steps_up = jnp.arange(1, degree_count + 1, dtype=jnp.float32)[None, :]
-    factor = jnp.where(
-        steps_up <= order_real, 0.5 * jnp.log((2.0 * steps_up + 1.0) / (2.0 * steps_up)), 0.0
-    )
-    log_start = 0.5 * jnp.log(1.0 / (4.0 * jnp.pi)) + jnp.sum(factor, axis=1, keepdims=True)
-    diagonal = jnp.exp(log_start + order_real * log_sine)
+LANES = 128
+
+
+def table_kernel(deg_ref, diag_ref, cos_ref, quad_ref, order_ref, q_ref, p_ref, slot_ref, rows_ref):
+    orders = diag_ref.shape[0]
+    lats = q_ref.shape[2]
+    degrees = deg_ref.shape[0]
+
+    def invert(slot, carry):
+        slot_ref[deg_ref[slot]] = slot
+        return carry
+
+    lax.fori_loop(0, degrees, invert, 0)
+    order_real = order_ref[...]
     squared = order_real * order_real
-
-    def advance(carry, degree):
+    diagonal = diag_ref[...]
+    cosine = cos_ref[...]
+    first_lead = jnp.sqrt(2.0 * order_real + 3.0)
+    halves = rows_ref.shape[0]
+
+    def advance(degree, carry):
         previous, older = carry
         degree_real = degree.astype(jnp.float32)
         lead = jnp.sqrt(
@@ -36,33 +42,64 @@
             jnp.maximum(lower * lower - squared, 0.0) / jnp.maximum(4.0 * lower * lower - 1.0, 1.0)
         )
         general = lead * (cosine * previous - back * older)
-        first = jnp.sqrt(2.0 * order_real + 3.0) * cosine * previous
+        first = first_lead * cosine * previous
         value = jnp.where(
-            degree == order_col,
+            degree_real == order_real,
             diagonal,
             jnp.where(
-                degree == order_col + 1, first, jnp.where(degree > order_col + 1, general, 0.0)
+                degree_real == order_real + 1.0,
+                first,
+                jnp.where(degree_real > order_real + 1.0, general, 0.0),
             ),
         )
-        return ((value, previous), value)
-
-    zeros = jnp.zeros((order_ids.shape[0], lat_count), jnp.float32)
-    final_state, table = lax.scan(
-        advance, (zeros, zeros), jnp.arange(degree_count, dtype=jnp.int32)
-    )
-    return jnp.transpose(table, (1, 0, 2))
+        slot = slot_ref[degree]
+        for half in range(halves):
+            rows_ref[half, pl.ds(slot, orders, stride=degrees), :] = value[
+                :, half * LANES : (half + 1) * LANES
+            ]
+        return (value, previous)
+
+    zeros = diagonal * 0.0
+    lax.fori_loop(0, degrees, advance, (zeros, zeros), unroll=4)
+    quadrature = quad_ref[...]
+    for order in range(orders):
+        for half in range(halves):
+            low = half * LANES
+            high = min(lats, low + LANES)
+            chosen = rows_ref[half, order * degrees : (order + 1) * degrees, :][:, : high - low]
+            p_ref[order, :, low:high] = chosen.astype(jnp.bfloat16)
+            q_ref[order, :, low:high] = (chosen * quadrature[:, low:high]).astype(jnp.bfloat16)
 
 
 def spectral_tables(start, ord_dev, degree_of):
-    order_ids = start + jnp.arange(ord_dev, dtype=jnp.int32)
-    mine = legendre_table(order_ids, LATS, DEGREES)
-    selector = (degree_of[:, None] == jnp.arange(DEGREES, dtype=jnp.int32)[None, :]).astype(
-        jnp.float32
-    )
-    chosen = jnp.einsum("mli,jl->mji", mine, selector, precision=lax.Precision.HIGHEST)
-    colatitude = jnp.pi * (jnp.arange(LATS, dtype=jnp.float32) + 0.5) / LATS
-    quadrature = 2.0 * jnp.pi * jnp.pi / LATS * jnp.sin(colatitude)
-    return ((chosen * quadrature[None, None, :]).astype(jnp.bfloat16), chosen.astype(jnp.bfloat16))
+    halves = -(-LATS // LANES)
+    padded = halves * LANES
+    order_col = (start + jnp.arange(ord_dev, dtype=jnp.int32)).astype(jnp.float32)[:, None]
+    lat_ids = jnp.minimum(jnp.arange(padded, dtype=jnp.float32), LATS - 1.0)
+    colatitude = jnp.pi * (lat_ids + 0.5) / LATS
+    sine = jnp.sin(colatitude)[None, :]
+    steps_up = jnp.arange(1, DEGREES + 1, dtype=jnp.float32)[None, :]
+    factor = jnp.where(
+        steps_up <= order_col, 0.5 * jnp.log((2.0 * steps_up + 1.0) / (2.0 * steps_up)), 0.0
+    )
+    log_start = 0.5 * jnp.log(1.0 / (4.0 * jnp.pi)) + jnp.sum(factor, axis=1, keepdims=True)
+    diagonal = jnp.exp(log_start + order_col * jnp.log(sine))
+    cosine = jnp.broadcast_to(jnp.cos(colatitude)[None, :], diagonal.shape)
+    quadrature = 2.0 * jnp.pi * jnp.pi / LATS * sine
+    orders = jnp.broadcast_to(order_col, diagonal.shape)
+    vmem = pl.BlockSpec(memory_space=pltpu.VMEM)
+    shape = jax.ShapeDtypeStruct((ord_dev, DEGREES, LATS), jnp.bfloat16)
+    return pl.pallas_call(
+        table_kernel,
+        out_shape=(shape, shape),
+        in_specs=[pl.BlockSpec(memory_space=pltpu.SMEM)] + [vmem] * 4,
+        out_specs=(vmem, vmem),
+        scratch_shapes=[
+            pltpu.SMEM((DEGREES,), jnp.int32),
+            pltpu.VMEM((halves, ord_dev * DEGREES, LANES), jnp.float32),
+        ],
+        name="legendre_tables",
+    )(degree_of, diagonal, cosine, quadrature, orders)
 
 
 def fourier_tables(lon_count, order_count):

time: 822 us -> 515 us (0.63)
  other arithmetic: 192 us -> 7.09 us
  loops' own time: 86.7 us -> 0 us
  local copies, waits for them, and re-layouts: 147 us -> 67.2 us
  waiting for transfers between devices: 127 us -> 173 us
    another operation x1 -> x0, loops' own time: 86.7 us -> none  [legendre_table(): lax.scan(advance, (zeros, zeros), jnp.arange(degree_count, dtype=jnp.int32))]
    gt x128 -> x0, other arithmetic: 82.3 us -> none  [advance(): degree > order_col + 1]
    eq x128 -> x0, other arithmetic: 81.4 us -> none  [advance(): degree == order_col]
    dynamic_slice x128 -> x0, local copies, waits for them, and re-layouts: 79.2 us -> none  [legendre_table(): lax.scan(advance, (zeros, zeros), jnp.arange(degree_count, dtype=jnp.int32))]
    all_to_all x1, waiting for transfers between devices: 0.01 us -> 45.9 us  [to_orders(): lax.all_to_all(values, 'lat', split_axis=1, concat_axis=0, tiled=True)]
    dynamic_update_slice x128 -> x0, other arithmetic: 11 us -> none  [legendre_table(): lax.scan(advance, (zeros, zeros), jnp.arange(degree_count, dtype=jnp.int32))]
  transfers between devices with their start and end apart: 5 -> 5, of which waited for: 3 -> 4; matrix products, arithmetic and copies ran while one was open for 35% -> 5% of each run, Pallas kernels for 0% -> 1%
where the time goes in v1:
time: 515 us; the launch traced here: 508 us
  blocking collectives  181 us (35%)
  waiting for transfers between devices  173 us (34%)
  local copies, waits for them, and re-layouts  67.2 us (13%)
  matrix products  36.4 us (7%)
  starting transfers between devices  23.6 us (5%)
  between operations  14.7 us (3%)
  other arithmetic  7.09 us (1%)
    all_to_all x2, waiting for transfers between devices, to_bands(): lax.all_to_all(values, 'lat', split_axis=0, concat_axis=1, tiled=True)  98.5 us
    all_to_all x2, blocking collectives, to_degrees(): lax.all_to_all(values, 'lat', split_axis=0, concat_axis=1, tiled=True)  82.3 us
    all_to_all x1, blocking collectives, to_orders(): lax.all_to_all(values, 'lat', split_axis=1, concat_axis=0, tiled=True)  57.6 us
    all_to_all x1, waiting for transfers between devices, to_orders(): lax.all_to_all(values, 'lat', split_axis=1, concat_axis=0, tiled=True)  45.9 us
    all_to_all x1, blocking collectives, back_to_orders(): lax.all_to_all(values, 'lat', split_axis=1, concat_axis=0, tiled=True)  40.8 us
    dot_general x19, matrix products, product(): return jnp.einsum(spec, left, right, preferred_element_type=jnp.float32)  36.4 us
    all_to_all x1, waiting for transfers between devices, back_to_orders(): lax.all_to_all(values, 'lat', split_axis=1, concat_axis=0, tiled=True)  28.6 us
    all_to_all x2, starting transfers between devices, to_bands(): lax.all_to_all(values, 'lat', split_axis=0, concat_axis=1, tiled=True)  10.7 us
  transfers between devices with their start and end apart: 5, of which 4 were waited for; matrix products, arithmetic and copies ran while one was open for 5% of the time, Pallas kernels for 1%

profile of v1, /device:TPU:12, one launch (start us, length us, event | category | flops | bytes accessed | tf_op | source)
XLA Modules:
  0.0 507.6 jit_solution(15613312227839985505)
XLA Ops:
  7.2 0.8 fusion.103
  8.0 0.7 fusion.94
  8.7 1.8 copy.194
  10.5 1.7 reshape.394
  12.2 3.7 convert_bitcast_fusion.3
  15.9 4.8 reshape.381
  20.7 3.0 copy.196
  23.8 7.2 %all-to-all-start = ((bf16[12,128,2,1,384]{4,2,0,3,1:T(2,128)(2,1)}), bf16[12,128,2,1,384]{4,2,0,3,1:T(2,128)(2,1)S(1)}, u32[]{:S(2)}, u32[]{:S(2)}) async-start(bf16[12,128,2,1,384]{4,2,0,3,1:T(2,128)(2,1)} %copy.196), calls=%async_computation | async-start | bytes 4718592 | tf_op jit(solution)/shard_map/all_to_all | solution.py:121
  31.1 0.6 sine_multiply_fusion.quad_ref
  31.9 0.7 add_exponential_fusion.diag_ref
  32.6 0.7 mul.178.order_ref
  33.2 0.6 broadcast_in_dim.39.cos_ref
  33.8 4.9 legendre_tables.1
  38.7 45.9 %all-to-all-done = bf16[12,128,2,1,384]{4,2,0,3,1:T(2,128)(2,1)S(1)} async-done(((bf16[12,128,2,1,384]{4,2,0,3,1:T(2,128)(2,1)}), bf16[12,128,2,1,384]{4,2,0,3,1:T(2,128)(2,1)S(1)}, u32[]{:S(2)}, u32[]{:S(2)}) %all-to-all-start) | async-done | bytes 2359328 | tf_op jit(solution)/shard_map/all_to_all | solution.py:121
  84.6 0.4 copy.280
  85.4 0.7 copy-done.4
  86.1 1.2 fusion.65
  87.4 2.9 copy.201
  90.3 41.2 %all_to_all.126 = bf16[128,8,2,1,384]{4,2,1,3,0:T(2,128)(2,1)S(1)} all-to-all(bf16[128,8,2,1,384]{4,2,1,3,0:T(2,128)(2,1)} %copy.201), channel_id=1, replica_groups=mesh['lat'=16,'batch'=2] {'lat'}, dimensions={0} | all-to-all | bytes 3145728 | tf_op jit(solution)/shard_map/all_to_all | solution.py:125
  132.0 0.7 fusion.26
  132.7 0.7 fusion.24
  133.4 0.7 fusion.76
  134.1 0.7 fusion.79
  135.0 0.9 copy.206
  135.9 40.8 %all_to_all.127 = bf16[8,128,2,1,384]{4,0,3,2,1:T(8,128)(2,1)S(1)} all-to-all(bf16[8,128,2,1,384]{4,0,3,2,1:T(8,128)(2,1)S(1)} %copy.206), channel_id=1, replica_groups=mesh['lat'=16,'batch'=2] {'lat'}, dimensions={1} | all-to-all | bytes 3145728 | tf_op jit(solution)/shard_map/all_to_all | solution.py:129
  176.7 0.8 convert_bitcast_fusion.2
  177.6 3.8 copy.209
  181.4 5.9 %all-to-all-start.3 = ((bf16[192,8,2,1,384]{4,2,1,3,0:T(2,128)(2,1)}), bf16[192,8,2,1,384]{4,2,1,3,0:T(2,128)(2,1)}, u32[]{:S(2)}, u32[]{:S(2)}) async-start(bf16[192,8,2,1,384]{4,2,1,3,0:T(2,128)(2,1)} %copy.209), calls=%async_computation.3 | async-start | bytes 4718592 | tf_op jit(solution)/shard_map/all_to_all | solution.py:133
  187.3 0.8 multiply_convert_fusion
  188.6 51.3 %all-to-all-done.3 = bf16[192,8,2,1,384]{4,2,1,3,0:T(2,128)(2,1)} async-done(((bf16[192,8,2,1,384]{4,2,1,3,0:T(2,128)(2,1)}), bf16[192,8,2,1,384]{4,2,1,3,0:T(2,128)(2,1)}, u32[]{:S(2)}, u32[]{:S(2)}) %all-to-all-start.3) | async-done | bytes 2359328 | tf_op jit(solution)/shard_map/all_to_all | solution.py:133
  239.8 2.1 copy.210
  242.0 3.8 copy.211
  245.8 6.1 %reshape.386 = bf16[12,256,384]{2,1,0:T(8,128)(2,1)} reshape(bf16[12,16,8,2,1,384]{5,3,2,1,0,4:T(2,128)(2,1)} %copy.211) | data formatting | bytes 4718592 | tf_op jit(solution)/shard_map/reshape.23
  251.9 9.2 %convert_bitcast_fusion.1 = bf16[12,256,1,384]{3,1,0,2:T(8,128)(2,1)} fusion(bf16[384,256,1]{0,1,2:T(8,128)(2,1)S(1)} %reshape.398, bf16[1,12,384,384]{3,2,1,0:T(8,128)(2,1)} %param.5, bf16[12,256,384]{2,1,0:T(8,128)(2,1)} %reshape.386, bf16[384,256]{0,1:T(8,128)(2,1)S(1)} %convert_element_type.143), kind=kOutput, calls=%fused_computation.49 | convolution fusion | flops 1850277888 | bytes 8650752 | tf_op jit(solution)/shard_map/sikc,fk->ifsc/dot_general | solution.py:137
  261.1 5.9 %reshape.388 = bf16[12,128,2,1,384]{4,2,1,0,3:T(2,128)(2,1)} reshape(bf16[12,256,1,384]{3,1,0,2:T(8,128)(2,1)} %convert_bitcast_fusion.1) | data formatting | bytes 4718592 | tf_op jit(solution)/shard_map/reshape | solution.py:191
  267.0 3.3 copy.213
  270.3 57.6 %all_to_all.128 = bf16[12,128,2,1,384]{4,2,0,3,1:T(2,128)(2,1)S(1)} all-to-all(bf16[12,128,2,1,384]{4,2,0,3,1:T(2,128)(2,1)S(1)} %copy.213), channel_id=1, replica_groups=mesh['lat'=16,'batch'=2] {'lat'}, dimensions={1} | all-to-all | bytes 4718592 | tf_op jit(solution)/shard_map/all_to_all | solution.py:121
  327.9 0.4 copy.279
  328.3 0.4 copy.215
  328.7 2.4 fusion.62
  331.1 4.9 copy.218
  336.0 41.2 %all_to_all.129 = bf16[128,8,2,1,384]{4,2,1,3,0:T(2,128)(2,1)S(1)} all-to-all(bf16[128,8,2,1,384]{4,2,1,3,0:T(2,128)(2,1)} %copy.218), channel_id=1, replica_groups=mesh['lat'=16,'batch'=2] {'lat'}, dimensions={0} | all-to-all | bytes 3145728 | tf_op jit(solution)/shard_map/all_to_all | solution.py:125
  377.8 0.9 fusion.22
  378.7 0.9 fusion.20
  379.6 0.9 fusion.82
  380.5 0.9 fusion.85
  381.6 2.1 copy.221
  383.7 5.5 %all-to-all-start.6 = ((bf16[8,128,2,1,384]{4,0,3,2,1:T(8,128)(2,1)}), bf16[8,128,2,1,384]{4,0,3,2,1:T(8,128)(2,1)}, u32[]{:S(2)}, u32[]{:S(2)}) async-start(bf16[8,128,2,1,384]{4,0,3,2,1:T(8,128)(2,1)} %copy.221), calls=%async_computation.6 | async-start | bytes 3145728 | tf_op jit(solution)/shard_map/all_to_all | solution.py:129
  389.4 2.1 fusion.93
  391.5 0.8 fusion.18
  392.3 0.8 fusion.92
  393.1 0.8 fusion.19
  393.9 2.7 pad_maximum_fusion
  396.7 28.6 %all-to-all-done.6 = bf16[8,128,2,1,384]{4,0,3,2,1:T(8,128)(2,1)} async-done(((bf16[8,128,2,1,384]{4,0,3,2,1:T(8,128)(2,1)}), bf16[8,128,2,1,384]{4,0,3,2,1:T(8,128)(2,1)}, u32[]{:S(2)}, u32[]{:S(2)}) %all-to-all-start.6) | async-done | bytes 1572896 | tf_op jit(solution)/shard_map/all_to_all | solution.py:129
  425.3 2.3 convert_bitcast_fusion
  427.6 3.8 copy.224
  431.4 4.8 all-to-all-start.7
  436.3 0.8 convert_element_type.142
  437.1 5.1 %copy.232 = bf16[8,2,384,384]{3,2,1,0:T(8,128)(2,1)} copy(bf16[8,2,384,384]{3,2,0,1:T(8,128)(2,1)} %all-reduce.2.cloned.1.call-done) | data formatting | bytes 9437184
  442.2 47.2 %all-to-all-done.7 = bf16[192,8,2,1,384]{4,2,1,3,0:T(2,128)(2,1)S(1)} async-done(((bf16[192,8,2,1,384]{4,2,1,3,0:T(2,128)(2,1)}), bf16[192,8,2,1,384]{4,2,1,3,0:T(2,128)(2,1)S(1)}, u32[]{:S(2)}, u32[]{:S(2)}) %all-to-all-start.7) | async-done | bytes 2359328 | tf_op jit(solution)/shard_map/all_to_all | solution.py:133
  489.4 0.5 copy.225
  489.9 2.4 copy.226
  492.3 2.4 reshape.393
  494.7 5.8 %fusion.10 = bf16[1,12,384,384]{3,2,1,0:T(8,128)(2,1)} fusion(bf16[1,12,384,384]{3,2,1,0:T(8,128)(2,1)} %param.5, bf16[12,256,384]{2,1,0:T(8,128)(2,1)} %reshape.393, bf16[384,256]{0,1:T(8,128)(2,1)} %convert_element_type.142), kind=kOutput, calls=%fused_computation.15 | convolution fusion | flops 911278080 | bytes 9633792 | tf_op jit(solution)/shard_map/ifsc,kf->sikc/dot_general | solution.py:137
  (45 shorter events, 2.8 us)
Async XLA Ops:
  7.2 5.0 copy-start
  23.8 60.9 %all-to-all-start = ((bf16[12,128,2,1,384]{4,2,0,3,1:T(2,128)(2,1)}), bf16[12,128,2,1,384]{4,2,0,3,1:T(2,128)(2,1)S(1)}, u32[]{:S(2)}, u32[]{:S(2)}) async-start(bf16[12,128,2,1,384]{4,2,0,3,1:T(2,128)(2,1)} %copy.196), calls=%async_computation | async-start | bytes 4718592 | tf_op jit(solution)/shard_map/all_to_all | solution.py:121
  85.1 1.0 copy-start.4
  86.1 45.9 %slice-start = ((s8[4718592]{0:T(1024)(128)(4,1)}), s8[524288]{0:T(1024)(128)(4,1)S(1)}, s32[]{:S(2)}) async-start(s8[4718592]{0:T(1024)(128)(4,1)} %bitcast.216), calls=%async_computation.9 | async-start | bytes 1048576
  90.3 41.7 %slice-start.1 = ((s8[4718592]{0:T(1024)(128)(4,1)}), s8[4194304]{0:T(1024)(128)(4,1)S(1)}, s32[]{:S(2)}) async-start(s8[4718592]{0:T(1024)(128)(4,1)} %bitcast.216), calls=%async_computation.10 | async-start | bytes 8388608
  135.9 40.8 %copy-start.5 = (bf16[8,128,192]{2,1,0:T(8,128)(2,1)S(1)}, bf16[8,128,192]{2,1,0:T(8,128)(2,1)}, u32[]{:S(2)}) copy-start(bf16[8,128,192]{2,1,0:T(8,128)(2,1)} %get-tuple-element.5) | copy-start | bytes 1179652
  181.4 58.4 %all-to-all-start.3 = ((bf16[192,8,2,1,384]{4,2,1,3,0:T(2,128)(2,1)}), bf16[192,8,2,1,384]{4,2,1,3,0:T(2,128)(2,1)}, u32[]{:S(2)}, u32[]{:S(2)}) async-start(bf16[192,8,2,1,384]{4,2,1,3,0:T(2,128)(2,1)} %copy.209), calls=%async_computation.3 | async-start | bytes 4718592 | tf_op jit(solution)/shard_map/all_to_all | solution.py:133
  328.7 49.0 %slice-start.2 = ((s8[4718592]{0:T(1024)(128)(4,1)}), s8[524288]{0:T(1024)(128)(4,1)S(1)}, s32[]{:S(2)}) async-start(s8[4718592]{0:T(1024)(128)(4,1)} %bitcast.218), calls=%async_computation.11 | async-start | bytes 1048576
  336.0 41.7 %slice-start.3 = ((s8[4718592]{0:T(1024)(128)(4,1)}), s8[4194304]{0:T(1024)(128)(4,1)S(1)}, s32[]{:S(2)}) async-start(s8[4718592]{0:T(1024)(128)(4,1)} %bitcast.218), calls=%async_computation.12 | async-start | bytes 8388608
  377.7 2.8 copy-start.2
  383.7 41.6 %all-to-all-start.6 = ((bf16[8,128,2,1,384]{4,0,3,2,1:T(8,128)(2,1)}), bf16[8,128,2,1,384]{4,0,3,2,1:T(8,128)(2,1)}, u32[]{:S(2)}, u32[]{:S(2)}) async-start(bf16[8,128,2,1,384]{4,0,3,2,1:T(8,128)(2,1)} %copy.221), calls=%async_computation.6 | async-start | bytes 3145728 | tf_op jit(solution)/shard_map/all_to_all | solution.py:129
  389.2 47.9 %all-reduce.2.cloned.1.call-start = ((), (), s32[]{:S(2)}) async-start(), calls=%async_computation.8 | async-start | bytes 9437184 | tf_op jit(solution)/shard_map/psum | solution.py:195
  389.4 2.1 copy-start.3
  431.4 4.8 copy-start.6
  431.4 58.0 %all-to-all-start.7 = ((bf16[192,8,2,1,384]{4,2,1,3,0:T(2,128)(2,1)}), bf16[192,8,2,1,384]{4,2,1,3,0:T(2,128)(2,1)S(1)}, u32[]{:S(2)}, u32[]{:S(2)}) async-start(bf16[192,8,2,1,384]{4,2,1,3,0:T(2,128)(2,1)} %copy.224), calls=%async_computation.7 | async-start | bytes 4718592 | tf_op jit(solution)/shard_map/all_to_all | solution.py:133
  494.7 5.8 %copy-start.1 = (bf16[1,12,384,384]{3,2,1,0:T(8,128)(2,1)S(1)}, bf16[1,12,384,384]{3,2,1,0:T(8,128)(2,1)}, u32[]{:S(2)}) copy-start(bf16[1,12,384,384]{3,2,1,0:T(8,128)(2,1)} %param.4) | copy-start | bytes 10616836
Sparse Core Ops, SparseCore 0:
  396.8 30.0 all-reduce.1

commit v2 on v1

--- a/solution.py
+++ b/solution.py
@@ -1,3 +1,5 @@
+import functools
+
 import jax
 import jax.numpy as jnp
 from jax import lax
@@ -167,6 +169,354 @@
     return jnp.stack([dw_real, dw_imag], axis=1)
 
 
+def pair_swap(values, even_sign):
+    rows = values.shape[0]
+    even = lax.broadcasted_iota(jnp.int32, values.shape, 0) % 2 == 0
+    above = pltpu.roll(values, rows - 1, 0)
+    below = pltpu.roll(values, 1, 0)
+    return jnp.where(even, even_sign * above, -even_sign * below)
+
+
+def gelu_slope(x):
+    scale = 0.7978845608028654
+    square = x * x
+    t = jnp.tanh(scale * (x + 0.044715 * x * square))
+    return 0.5 * (1.0 + t) + 0.5 * x * (1.0 - t * t) * (scale * (1.0 + 0.134145 * square))
+
+
+def dot(left, right, dims=((1,), (0,))):
+    return lax.dot_general(left, right, (dims, ((), ())), preferred_element_type=jnp.float32)
+
+
+def block_kernel(
+    n, nb, fields, cotangent, weights, qtab, ptab, fwd_fk, fwd_kf, inv_fk, inv_kf,
+    grad_out, dw_out,
+    fbuf, cbuf, wbuf, band_out, band_in, ord_in, ord_out, deg_out, deg_back, co, go, mixed,
+    wide_a, wide_b, dw, dw_in,
+    load_sem, send_sem, recv_sem, dw_send, dw_recv, out_sem,
+):
+    me = lax.axis_index("lat")
+    me_b = lax.axis_index("batch")
+    chunks, lat_dev = fbuf.shape[0], fbuf.shape[1]
+    orders = qtab.shape[0]
+    rows = 2 * orders
+    slots = co.shape[1]
+    degrees = n * slots
+    lats = n * lat_dev
+    mesh_id = pl.DeviceIdType.MESH
+
+    def lanes(chunk):
+        return pl.ds(chunk * LANES, LANES)
+
+    def load(chunk):
+        return pltpu.make_async_copy(
+            fields.at[0, :, :, lanes(chunk)], fbuf.at[chunk], load_sem.at[chunk]
+        )
+
+    def load_cot(chunk):
+        return pltpu.make_async_copy(
+            cotangent.at[0, :, :, lanes(chunk)], cbuf.at[chunk], load_sem.at[chunks + chunk]
+        )
+
+    load_w = pltpu.make_async_copy(weights, wbuf, load_sem.at[2 * chunks])
+    for chunk in range(chunks):
+        load(chunk).start()
+    load_w.start()
+    for chunk in range(chunks):
+        load_cot(chunk).start()
+
+    barrier = pltpu.get_barrier_semaphore()
+
+    def greet(step, carry):
+        peer = lax.rem(me + step, n)
+        pl.semaphore_signal(barrier, inc=1, device_id={"lat": peer}, device_id_type=mesh_id)
+        return carry
+
+    lax.fori_loop(1, n, greet, 0)
+    for step in range(1, nb):
+        peer = lax.rem(me_b + step, nb)
+        pl.semaphore_signal(barrier, inc=1, device_id={"batch": peer}, device_id_type=mesh_id)
+    pl.semaphore_wait(barrier, n - 1 + nb - 1)
+
+    def part(ref, chunk, kind, owner):
+        if kind == "band":
+            return ref.at[chunk, :, pl.ds(pl.multiple_of(owner * rows, rows), rows), :]
+        if kind == "lat":
+            return ref.at[chunk, pl.ds(owner * lat_dev, lat_dev)]
+        return ref.at[chunk, pl.ds(owner * slots, slots)]
+
+    def exchange(stage, chunk, source, source_kind, target, target_kind):
+        def send(step, carry):
+            peer = lax.rem(me + step, n)
+            pltpu.make_async_remote_copy(
+                src_ref=part(source, chunk, source_kind, peer),
+                dst_ref=part(target, chunk, target_kind, me),
+                send_sem=send_sem.at[stage, chunk],
+                recv_sem=recv_sem.at[stage, chunk],
+                device_id={"lat": peer},
+                device_id_type=mesh_id,
+            ).start()
+            return carry
+
+        lax.fori_loop(1, n, send, 0)
+        pltpu.make_async_copy(
+            part(source, chunk, source_kind, me),
+            part(target, chunk, target_kind, me),
+            recv_sem.at[stage, chunk],
+        ).start()
+
+    def arrived(stage, chunk, target):
+        pltpu.make_async_copy(target.at[chunk], target.at[chunk], recv_sem.at[stage, chunk]).wait()
+
+    def departed(stage, chunk, source, kind):
+        if kind == "band":
+            view = source.at[chunk, :, 0 : (n - 1) * rows, :]
+        elif kind == "lat":
+            view = source.at[chunk, 0 : (n - 1) * lat_dev]
+        else:
+            view = source.at[chunk, 0 : (n - 1) * slots]
+        pltpu.make_async_copy(view, view, send_sem.at[stage, chunk]).wait()
+
+    def widen(source, chunk, depth):
+        def one(block, carry):
+            piece = source[chunk, pl.ds(block * depth, depth)].astype(jnp.float32)
+            wide_a[pl.ds(pl.multiple_of(block * depth * rows, depth * rows), depth * rows), :] = (
+                piece.reshape(depth * rows, LANES)
+            )
+            return carry
+
+        lax.fori_loop(0, n, one, 0)
+
+    def narrow(target, chunk, depth):
+        def one(block, carry):
+            start = pl.multiple_of(block * depth * rows, depth * rows)
+            piece = wide_b[pl.ds(start, depth * rows), :]
+            target[chunk, pl.ds(block * depth, depth)] = piece.reshape(
+                depth, rows, LANES
+            ).astype(jnp.bfloat16)
+            return carry
+
+        lax.fori_loop(0, n, one, 0)
+
+    def apply_table(table, depth_in, depth_out, dims):
+        def one(order, carry):
+            real = wide_a[pl.ds(2 * order, depth_in, stride=rows), :]
+            imag = wide_a[pl.ds(2 * order + 1, depth_in, stride=rows), :]
+            both = jnp.concatenate([real, imag], axis=1).astype(jnp.bfloat16)
+            result = dot(table[order], both, dims)
+            wide_b[pl.ds(2 * order, depth_out, stride=rows), :] = result[:, :LANES]
+            wide_b[pl.ds(2 * order + 1, depth_out, stride=rows), :] = result[:, LANES:]
+            return carry
+
+        lax.fori_loop(0, orders, one, 0)
+
+    def analyse(stage, chunk, table, target, before):
+        arrived(stage, chunk, ord_in)
+        widen(ord_in, chunk, lat_dev)
+        apply_table(table, lats, degrees, ((1,), (0,)))
+        if before is not None:
+            departed(before, chunk, deg_out, "slot")
+        narrow(deg_out, chunk, slots)
+        exchange(stage + 1, chunk, deg_out, "slot", target, "band")
+
+    def synthesise(stage, chunk, table, before):
+        arrived(stage, chunk, deg_back)
+        widen(deg_back, chunk, slots)
+        apply_table(table, degrees, lats, ((0,), (0,)))
+        if before is not None:
+            departed(before, chunk, ord_out, "lat")
+        narrow(ord_out, chunk, lat_dev)
+        exchange(stage + 1, chunk, ord_out, "lat", band_in, "band")
+
+    def joined(source, slot):
+        return jnp.concatenate([source[chunk, slot] for chunk in range(chunks)], axis=1)
+
+    for chunk in range(chunks):
+        load(chunk).wait()
+
+        def fourier(row, carry):
+            band_out[chunk, row] = dot(fwd_fk[...], fbuf[chunk, row]).astype(jnp.bfloat16)
+            return carry
+
+        lax.fori_loop(0, lat_dev, fourier, 0)
+        exchange(0, chunk, band_out, "band", ord_in, "lat")
+    for chunk in range(chunks):
+        analyse(0, chunk, qtab, co, None)
+    load_w.wait()
+    for chunk in range(chunks):
+        arrived(1, chunk, co)
+    for chunk in range(chunks):
+
+        def mix(slot, carry):
+            values = joined(co, slot)
+            same = dot(values, wbuf[slot, 0, :, chunk * LANES : (chunk + 1) * LANES])
+            cross = dot(values, wbuf[slot, 1, :, chunk * LANES : (chunk + 1) * LANES])
+            mixed[chunk, slot] = (same + pair_swap(cross, -1.0)).astype(jnp.bfloat16)
+            return carry
+
+        lax.fori_loop(0, slots, mix, 0)
+        exchange(2, chunk, mixed, "band", deg_back, "slot")
+    for chunk in range(chunks):
+        synthesise(2, chunk, ptab, None)
+    for chunk in range(chunks):
+        load_cot(chunk).wait()
+        arrived(3, chunk, band_in)
+        departed(0, chunk, band_out, "band")
+
+        def middle(row, carry):
+            response = dot(inv_kf[...], band_in[chunk, row])
+            upstream = cbuf[chunk, row].astype(jnp.float32) * gelu_slope(response)
+            band_out[chunk, row] = dot(inv_fk[...], upstream.astype(jnp.bfloat16)).astype(
+                jnp.bfloat16
+            )
+            return carry
+
+        lax.fori_loop(0, lat_dev, middle, 0)
+        exchange(4, chunk, band_out, "band", ord_in, "lat")
+    for chunk in range(chunks):
+        analyse(4, chunk, ptab, go, 1)
+    for chunk in range(chunks):
+        arrived(5, chunk, go)
+    for chunk in range(chunks):
+        departed(2, chunk, mixed, "band")
+
+        def adjoint(slot, carry):
+            values = joined(go, slot)
+            span = ((1,), (1,))
+            same = dot(values, wbuf[slot, 0, chunk * LANES : (chunk + 1) * LANES, :], span)
+            cross = dot(values, wbuf[slot, 1, chunk * LANES : (chunk + 1) * LANES, :], span)
+            mixed[chunk, slot] = (same + pair_swap(cross, 1.0)).astype(jnp.bfloat16)
+            return carry
+
+        lax.fori_loop(0, slots, adjoint, 0)
+        exchange(6, chunk, mixed, "band", deg_back, "slot")
+
+    def weight_grad(slot, carry):
+        values = joined(co, slot)
+        grads = joined(go, slot)
+        turned = pair_swap(grads.astype(jnp.float32), 1.0).astype(jnp.bfloat16)
+        span = ((0,), (0,))
+        dw[slot, 0] = dot(values, grads, span).astype(jnp.bfloat16)
+        dw[slot, 1] = dot(values, turned, span).astype(jnp.bfloat16)
+        return carry
+
+    lax.fori_loop(0, slots, weight_grad, 0)
+    dw_copies = []
+    for step in range(1, nb):
+        peer = lax.rem(me_b + step, nb)
+        copy = pltpu.make_async_remote_copy(
+            src_ref=dw,
+            dst_ref=dw_in.at[step - 1],
+            send_sem=dw_send.at[step - 1],
+            recv_sem=dw_recv.at[step - 1],
+            device_id={"batch": peer},
+            device_id_type=mesh_id,
+        )
+        copy.start()
+        dw_copies.append(copy)
+    for chunk in range(chunks):
+        synthesise(6, chunk, qtab, 3)
+    for copy in dw_copies:
+        copy.wait()
+
+    def total(slot, carry):
+        value = dw[slot].astype(jnp.float32)
+        for step in range(nb - 1):
+            value = value + dw_in[step, slot].astype(jnp.float32)
+        dw[slot] = value.astype(jnp.bfloat16)
+        return carry
+
+    lax.fori_loop(0, slots, total, 0)
+    store_w = pltpu.make_async_copy(dw, dw_out, out_sem.at[chunks])
+    store_w.start()
+
+    def store(chunk):
+        return pltpu.make_async_copy(
+            cbuf.at[chunk], grad_out.at[0, :, :, lanes(chunk)], out_sem.at[chunk]
+        )
+
+    for chunk in range(chunks):
+        arrived(7, chunk, band_in)
+
+        def finish(row, carry):
+            delta = dot(fwd_kf[...], band_in[chunk, row])
+            cbuf[chunk, row] = (cbuf[chunk, row].astype(jnp.float32) + delta).astype(jnp.bfloat16)
+            return carry
+
+        lax.fori_loop(0, lat_dev, finish, 0)
+        store(chunk).start()
+    for chunk in range(chunks):
+        departed(4, chunk, band_out, "band")
+        departed(5, chunk, deg_out, "slot")
+        departed(6, chunk, mixed, "band")
+        departed(7, chunk, ord_out, "lat")
+        store(chunk).wait()
+    store_w.wait()
+
+
+def local_kernel(fields, cotangent, weights, degree_of):
+    if fields.shape[0] != 1:
+        return local(fields, cotangent, weights, degree_of)
+    n = lax.axis_size("lat")
+    nb = lax.axis_size("batch")
+    lat_dev, lons, channels = fields.shape[1:]
+    slots = weights.shape[0]
+    orders = ORDERS // n
+    rows = 2 * orders
+    chunks = channels // LANES
+    forward, inverse = fourier_tables(LONS, ORDERS)
+    qtab, ptab = spectral_tables(lax.axis_index("lat") * orders, orders, degree_of)
+    vmem = pl.BlockSpec(memory_space=pltpu.VMEM)
+    anywhere = pl.BlockSpec(memory_space=pl.ANY)
+
+    def buffer(*dims):
+        return pltpu.VMEM(dims, jnp.bfloat16)
+
+    dma = pltpu.SemaphoreType.DMA
+    others = max(nb - 1, 1)
+    wide_rows = max(LATS, DEGREES) * rows
+    return pl.pallas_call(
+        functools.partial(block_kernel, n, nb),
+        out_shape=(
+            jax.ShapeDtypeStruct(fields.shape, jnp.bfloat16),
+            jax.ShapeDtypeStruct(weights.shape, jnp.bfloat16),
+        ),
+        in_specs=[anywhere] * 3 + [vmem] * 6,
+        out_specs=(anywhere, anywhere),
+        scratch_shapes=[
+            buffer(chunks, lat_dev, lons, LANES),
+            buffer(chunks, lat_dev, lons, LANES),
+            buffer(*weights.shape),
+            buffer(chunks, lat_dev, n * rows, LANES),
+            buffer(chunks, lat_dev, n * rows, LANES),
+            buffer(chunks, LATS, rows, LANES),
+            buffer(chunks, LATS, rows, LANES),
+            buffer(chunks, DEGREES, rows, LANES),
+            buffer(chunks, DEGREES, rows, LANES),
+            buffer(chunks, slots, n * rows, LANES),
+            buffer(chunks, slots, n * rows, LANES),
+            buffer(chunks, slots, n * rows, LANES),
+            pltpu.VMEM((wide_rows, LANES), jnp.float32),
+            pltpu.VMEM((wide_rows, LANES), jnp.float32),
+            buffer(*weights.shape),
+            buffer(others, *weights.shape),
+            dma((2 * chunks + 1,)),
+            dma((8, chunks)),
+            dma((8, chunks)),
+            dma((others,)),
+            dma((others,)),
+            dma((chunks + 1,)),
+        ],
+        compiler_params=pltpu.CompilerParams(
+            collective_id=0, has_side_effects=True, vmem_limit_bytes=60 * 2**20
+        ),
+        name="filter_block",
+    )(
+        fields, cotangent, weights, qtab, ptab,
+        jnp.transpose(forward), forward, inverse, jnp.transpose(inverse),
+    )
+
+
 def local(fields, cotangent, weights, degree_of):
     samples = fields.shape[0]
     band_rows = fields.shape[1]
@@ -205,8 +555,9 @@
 
 
 def solution(mesh):
+    orders = ORDERS // mesh.shape["lat"]
     return jax.shard_map(
-        local,
+        local_kernel if orders % 8 == 0 and CHANNELS % LANES == 0 else local,
         mesh=mesh,
         in_specs=(
             P("batch", "lat", None, None),

time: 515 us -> 376 us (0.73); the launches traced: 508 us -> 375 us
  Pallas kernels: 4.9 us -> 361 us
  blocking collectives: 181 us -> 0 us
  waiting for transfers between devices: 173 us -> 0 us
  local copies, waits for them, and re-layouts: 67.2 us -> 9.98 us
  matrix products: 36.4 us -> 0 us
  starting transfers between devices: 23.6 us -> 0 us
  between operations: 14.7 us -> 0.76 us
    pallas_call x0 -> x1, Pallas kernels: none -> 356 us  [local_kernel(): pl.pallas_call(functools.partial(block_kernel, n, nb), out_shape=(jax.Sha...]
    all_to_all x4 -> x0, blocking collectives: 181 us -> none  [the longest x2 82.3 us: to_degrees(): lax.all_to_all(values, 'lat', split_axis=0, concat_axis=1, tiled=True)]
    all_to_all x4 -> x0, waiting for transfers between devices: 173 us -> none  [the longest x2 98.5 us: to_bands(): lax.all_to_all(values, 'lat', split_axis=0, concat_axis=1, tiled=True)]
    dot_general x19 -> x0, matrix products: 36.4 us -> none  [product(): return jnp.einsum(spec, left, right, preferred_element_type=jnp.float32)]
    all_to_all x4 -> x0, starting transfers between devices: 23.4 us -> none  [the longest x2 10.7 us: to_bands(): lax.all_to_all(values, 'lat', split_axis=0, concat_axis=1, tiled=True)]
    reshape x4 -> x0, local copies, waits for them, and re-layouts: 17.1 us -> none  [the longest x2 9.21 us: local(): grad_synth = grad_synth.reshape(band_rows, ORDERS, 2, samples, CHANNELS)]
    convert_element_type x4 -> x0, local copies, waits for them, and re-layouts: 15.5 us -> none  [the longest x1 4.91 us: local(): product('mji,imrsc->jmrsc', pslot, grad_gathered).astype(jnp.bfloat16)]
    another operation x5 -> x0, local copies, waits for them, and re-layouts: 11.6 us -> none
  transfers between devices with their start and end apart: 5 -> 0, of which waited for: 4 -> 0; matrix products, arithmetic and copies ran while one was open for 5% -> 0% of each run, Pallas kernels for 1% -> 0%
where the time goes in v2:
time: 376 us; the launch traced here: 375 us
  Pallas kernels  361 us (96%)
  local copies, waits for them, and re-layouts  9.98 us (3%)
    pallas_call x1, Pallas kernels, local_kernel(): pl.pallas_call(functools.partial(block_kernel, n, nb), out_shape=(jax.Sha...  356 us

profile of v2, /device:TPU:12, one launch (start us, length us, event | category | flops | bytes accessed | tf_op | source)
XLA Modules:
  0.0 375.0 jit_solution(17800564353631236597)
XLA Ops:
  0.8 0.6 sine_multiply_fusion.quad_ref
  1.4 0.2 select_reduce_fusion
  1.6 0.7 add_exponential_fusion.diag_ref
  2.3 0.6 broadcast_in_dim.20.cos_ref
  2.9 0.7 mul.130.order_ref
  3.6 0.8 fusion.7
  4.4 0.2 copy.13
  4.6 0.1 convert_element_type.52
  4.7 0.0 copy-start.1
  4.7 0.8 copy.15.inv_kf
  5.6 0.8 fusion.6
  6.4 0.2 copy.12
  6.6 0.1 convert_element_type.50
  6.7 0.0 copy-start.2
  6.7 0.8 copy.14.fwd_kf
  7.6 4.9 %legendre_tables.1 = (bf16[8,128,192]{2,1,0:T(8,128)(2,1)}, bf16[8,128,192]{2,1,0:T(8,128)(2,1)}) custom-call(s32[128]{0:T(128)} %deg_ref.1, f32[8,256]{1,0:T(8,128)} %add_exponential_fusion.diag_ref, f32[8,256]{1,0:T(8,128)} %broadcast_in_dim.20.cos_ref, f32[1,256]{1,0:T(1,128)} %sine_multiply_fusion.quad_ref, f32[8,256]{1,0:T(8,128)} %mul.130.order_ref), custom_call_target="tpu_custom_call" | custom-call | tf_op jit(solution)/shard_map/legendre_tables/pallas_call | solution.py:94
  12.5 0.0 copy-done.1
  12.5 0.0 copy-done.2
  12.5 356.1 %filter_block.1 = (bf16[1,12,384,384]{3,2,1,0:T(8,128)(2,1)}, bf16[8,2,384,384]{3,2,1,0:T(8,128)(2,1)}) custom-call(bf16[1,12,384,384]{3,2,1,0:T(8,128)(2,1)} %fields.1, bf16[1,12,384,384]{3,2,1,0:T(8,128)(2,1)} %cotangent.1, bf16[8,2,384,384]{3,2,1,0:T(8,128)(2,1)} %weights.1, bf16[8,128,192]{2,1,0:T(8,128)(2,1)} %get-tuple-element.4.qtab, ...), custom_call_target="tpu_custom_call" | custom-call | tf_op jit(solution)/shard_map/filter_block/pallas_call | solution.py:478
  368.5 0.0 copy-start
  368.5 4.3 %copy.18 = bf16[1,12,384,384]{3,2,1,0:T(8,128)(2,1)} copy(bf16[1,12,384,384]{3,2,1,0:T(8,128)(2,1)} %get-tuple-element.14) | data formatting | bytes 7077888
  372.9 0.0 copy-done
  372.9 2.2 copy.19
  (9 shorter events, 0.2 us)
Async XLA Ops:
  4.7 7.7 %copy-start.1 = (bf16[384,256]{0,1:T(8,128)(2,1)}, bf16[384,256]{0,1:T(8,128)(2,1)S(1)}, u32[]{:S(2)}) copy-start(bf16[384,256]{0,1:T(8,128)(2,1)S(1)} %convert_element_type.52) | copy-start | bytes 589828
  6.7 5.8 %copy-start.2 = (bf16[384,256]{0,1:T(8,128)(2,1)}, bf16[384,256]{0,1:T(8,128)(2,1)S(1)}, u32[]{:S(2)}) copy-start(bf16[384,256]{0,1:T(8,128)(2,1)S(1)} %convert_element_type.50) | copy-start | bytes 589828
  368.5 4.3 %copy-start = (bf16[8,2,384,384]{3,2,1,0:T(8,128)(2,1)S(1)}, bf16[8,2,384,384]{3,2,1,0:T(8,128)(2,1)}, u32[]{:S(2)}) copy-start(bf16[8,2,384,384]{3,2,1,0:T(8,128)(2,1)} %get-tuple-element.15) | copy-start | bytes 14155780

commit v3 on v2

--- a/solution.py
+++ b/solution.py
@@ -1,6 +1,7 @@
 import functools
 
 import jax
+import numpy as np
 import jax.numpy as jnp
 from jax import lax
 from jax.experimental import pallas as pl
@@ -169,6 +170,84 @@
     return jnp.stack([dw_real, dw_imag], axis=1)
 
 
+def constant_tables(orders):
+    padded = -(-LATS // LANES) * LANES
+    lat_ids = np.minimum(np.arange(padded), LATS - 1)
+    colatitude = np.pi * (lat_ids + 0.5) / LATS
+    sine = np.sin(colatitude)[None, :]
+    ids = np.arange(ORDERS)
+    steps_up = np.arange(1, ORDERS + 1)
+    growth = np.cumsum(0.5 * np.log((2.0 * steps_up + 1.0) / (2.0 * steps_up)))
+    log_start = 0.5 * np.log(1.0 / (4.0 * np.pi)) + np.concatenate([[0.0], growth[:-1]])
+    diagonal = np.exp(log_start[:, None] + ids[:, None] * np.log(sine))
+    cosine = np.broadcast_to(np.cos(colatitude)[None, :], (orders, padded))
+    quadrature = 2.0 * np.pi * np.pi / LATS * sine
+    phase = 2.0 * np.pi * (np.arange(LONS)[:, None] * ids[None, :] % LONS) / LONS
+    forward = np.stack([np.cos(phase), -np.sin(phase)], axis=2).reshape(LONS, -1) / LONS
+    doubled = np.where(ids == 0, 1.0, 2.0)[None, :]
+    inverse = np.stack([doubled * np.cos(phase), -doubled * np.sin(phase)], axis=2)
+    inverse = inverse.reshape(LONS, -1)
+    floats = [jnp.asarray(t, jnp.float32) for t in (diagonal, cosine, quadrature)]
+    waves = [forward.T, forward, inverse.T, inverse]
+    halves = [jnp.asarray(np.float32(t).astype(jnp.bfloat16)) for t in waves]
+    return floats, halves
+
+
+def fill_tables(first_order, deg_ref, diag_ref, cos_ref, quad_ref, qtab, ptab, table, by_slot):
+    orders, degrees, lats = qtab.shape
+    halves = by_slot.shape[0]
+    diagonal = diag_ref[pl.ds(pl.multiple_of(first_order, orders), orders), :]
+    cosine = cos_ref[...]
+    order_ids = first_order + lax.broadcasted_iota(jnp.int32, diagonal.shape, 0)
+    order_real = order_ids.astype(jnp.float32)
+    squared = order_real * order_real
+    first_lead = jnp.sqrt(2.0 * order_real + 3.0)
+
+    def advance(degree, carry):
+        previous, older = carry
+        degree_real = degree.astype(jnp.float32)
+        lead = jnp.sqrt(
+            jnp.maximum(4.0 * degree_real * degree_real - 1.0, 0.0)
+            / jnp.maximum(degree_real * degree_real - squared, 1.0)
+        )
+        lower = degree_real - 1.0
+        back = jnp.sqrt(
+            jnp.maximum(lower * lower - squared, 0.0) / jnp.maximum(4.0 * lower * lower - 1.0, 1.0)
+        )
+        general = lead * (cosine * previous - back * older)
+        first = first_lead * cosine * previous
+        value = jnp.where(
+            order_ids == degree,
+            diagonal,
+            jnp.where(
+                order_ids + 1 == degree, first, jnp.where(order_ids + 1 < degree, general, 0.0)
+            ),
+        )
+        table[degree] = value
+        return (value, previous)
+
+    zeros = diagonal * 0.0
+    lax.fori_loop(0, degrees, advance, (zeros, zeros), unroll=2)
+
+    def place(slot, carry):
+        value = table[deg_ref[slot]]
+        for half in range(halves):
+            by_slot[half, pl.ds(slot, orders, stride=degrees), :] = value[
+                :, half * LANES : (half + 1) * LANES
+            ]
+        return carry
+
+    lax.fori_loop(0, degrees, place, 0)
+    quadrature = quad_ref[...]
+    for order in range(orders):
+        for half in range(halves):
+            low = half * LANES
+            high = min(lats, low + LANES)
+            chosen = by_slot[half, order * degrees : (order + 1) * degrees, :][:, : high - low]
+            ptab[order, :, low:high] = chosen.astype(jnp.bfloat16)
+            qtab[order, :, low:high] = (chosen * quadrature[:, low:high]).astype(jnp.bfloat16)
+
+
 def pair_swap(values, even_sign):
     rows = values.shape[0]
     even = lax.broadcasted_iota(jnp.int32, values.shape, 0) % 2 == 0
@@ -189,10 +268,11 @@
 
 
 def block_kernel(
-    n, nb, fields, cotangent, weights, qtab, ptab, fwd_fk, fwd_kf, inv_fk, inv_kf,
+    n, nb, fields, cotangent, weights, deg_ref, diag_ref, cos_ref, quad_ref,
+    fwd_fk, fwd_kf, inv_fk, inv_kf,
     grad_out, dw_out,
     fbuf, cbuf, wbuf, band_out, band_in, ord_in, ord_out, deg_out, deg_back, co, go, mixed,
-    wide_a, wide_b, dw, dw_in,
+    wide_a, wide_b, dw, dw_in, qtab, ptab, table, by_slot,
     load_sem, send_sem, recv_sem, dw_send, dw_recv, out_sem,
 ):
     me = lax.axis_index("lat")
@@ -247,7 +327,7 @@
 
     def exchange(stage, chunk, source, source_kind, target, target_kind):
         def send(step, carry):
-            peer = lax.rem(me + step, n)
+            peer = lax.rem(me + 1 + lax.rem(step + n // 2 - 2, n - 1), n)
             pltpu.make_async_remote_copy(
                 src_ref=part(source, chunk, source_kind, peer),
                 dst_ref=part(target, chunk, target_kind, me),
@@ -328,6 +408,14 @@
         narrow(ord_out, chunk, lat_dev)
         exchange(stage + 1, chunk, ord_out, "lat", band_in, "band")
 
+    def pair(source, chunk, row):
+        return jnp.concatenate([source[chunk, 2 * row], source[chunk, 2 * row + 1]], axis=1)
+
+    def put_pair(target, chunk, row, values):
+        values = values.astype(jnp.bfloat16)
+        target[chunk, 2 * row] = values[:, :LANES]
+        target[chunk, 2 * row + 1] = values[:, LANES:]
+
     def joined(source, slot):
         return jnp.concatenate([source[chunk, slot] for chunk in range(chunks)], axis=1)
 
@@ -335,11 +423,14 @@
         load(chunk).wait()
 
         def fourier(row, carry):
-            band_out[chunk, row] = dot(fwd_fk[...], fbuf[chunk, row]).astype(jnp.bfloat16)
-            return carry
-
-        lax.fori_loop(0, lat_dev, fourier, 0)
+            put_pair(band_out, chunk, row, dot(fwd_fk[...], pair(fbuf, chunk, row)))
+            return carry
+
+        lax.fori_loop(0, lat_dev // 2, fourier, 0)
         exchange(0, chunk, band_out, "band", ord_in, "lat")
+    fill_tables(
+        me * orders, deg_ref, diag_ref, cos_ref, quad_ref, qtab, ptab, table, by_slot
+    )
     for chunk in range(chunks):
         analyse(0, chunk, qtab, co, None)
     load_w.wait()
@@ -349,9 +440,12 @@
 
         def mix(slot, carry):
             values = joined(co, slot)
-            same = dot(values, wbuf[slot, 0, :, chunk * LANES : (chunk + 1) * LANES])
-            cross = dot(values, wbuf[slot, 1, :, chunk * LANES : (chunk + 1) * LANES])
-            mixed[chunk, slot] = (same + pair_swap(cross, -1.0)).astype(jnp.bfloat16)
+            span = slice(chunk * LANES, (chunk + 1) * LANES)
+            both = dot(
+                values, jnp.concatenate([wbuf[slot, 0, :, span], wbuf[slot, 1, :, span]], axis=1)
+            )
+            crossed = pair_swap(both[:, LANES:], -1.0)
+            mixed[chunk, slot] = (both[:, :LANES] + crossed).astype(jnp.bfloat16)
             return carry
 
         lax.fori_loop(0, slots, mix, 0)
@@ -364,14 +458,12 @@
         departed(0, chunk, band_out, "band")
 
         def middle(row, carry):
-            response = dot(inv_kf[...], band_in[chunk, row])
-            upstream = cbuf[chunk, row].astype(jnp.float32) * gelu_slope(response)
-            band_out[chunk, row] = dot(inv_fk[...], upstream.astype(jnp.bfloat16)).astype(
-                jnp.bfloat16
-            )
-            return carry
-
-        lax.fori_loop(0, lat_dev, middle, 0)
+            response = dot(inv_kf[...], pair(band_in, chunk, row))
+            upstream = pair(cbuf, chunk, row).astype(jnp.float32) * gelu_slope(response)
+            put_pair(band_out, chunk, row, dot(inv_fk[...], upstream.astype(jnp.bfloat16)))
+            return carry
+
+        lax.fori_loop(0, lat_dev // 2, middle, 0)
         exchange(4, chunk, band_out, "band", ord_in, "lat")
     for chunk in range(chunks):
         analyse(4, chunk, ptab, go, 1)
@@ -382,10 +474,14 @@
 
         def adjoint(slot, carry):
             values = joined(go, slot)
-            span = ((1,), (1,))
-            same = dot(values, wbuf[slot, 0, chunk * LANES : (chunk + 1) * LANES, :], span)
-            cross = dot(values, wbuf[slot, 1, chunk * LANES : (chunk + 1) * LANES, :], span)
-            mixed[chunk, slot] = (same + pair_swap(cross, 1.0)).astype(jnp.bfloat16)
+            span = slice(chunk * LANES, (chunk + 1) * LANES)
+            both = dot(
+                values,
+                jnp.concatenate([wbuf[slot, 0, span, :], wbuf[slot, 1, span, :]], axis=0),
+                ((1,), (1,)),
+            )
+            crossed = pair_swap(both[:, LANES:], 1.0)
+            mixed[chunk, slot] = (both[:, :LANES] + crossed).astype(jnp.bfloat16)
             return carry
 
         lax.fori_loop(0, slots, adjoint, 0)
@@ -439,11 +535,11 @@
         arrived(7, chunk, band_in)
 
         def finish(row, carry):
-            delta = dot(fwd_kf[...], band_in[chunk, row])
-            cbuf[chunk, row] = (cbuf[chunk, row].astype(jnp.float32) + delta).astype(jnp.bfloat16)
-            return carry
-
-        lax.fori_loop(0, lat_dev, finish, 0)
+            delta = dot(fwd_kf[...], pair(band_in, chunk, row))
+            put_pair(cbuf, chunk, row, pair(cbuf, chunk, row).astype(jnp.float32) + delta)
+            return carry
+
+        lax.fori_loop(0, lat_dev // 2, finish, 0)
         store(chunk).start()
     for chunk in range(chunks):
         departed(4, chunk, band_out, "band")
@@ -455,7 +551,7 @@
 
 
 def local_kernel(fields, cotangent, weights, degree_of):
-    if fields.shape[0] != 1:
+    if fields.shape[0] != 1 or fields.shape[1] % 2:
         return local(fields, cotangent, weights, degree_of)
     n = lax.axis_size("lat")
     nb = lax.axis_size("batch")
@@ -464,8 +560,8 @@
     orders = ORDERS // n
     rows = 2 * orders
     chunks = channels // LANES
-    forward, inverse = fourier_tables(LONS, ORDERS)
-    qtab, ptab = spectral_tables(lax.axis_index("lat") * orders, orders, degree_of)
+    floats, waves = constant_tables(orders)
+    halves = -(-LATS // LANES)
     vmem = pl.BlockSpec(memory_space=pltpu.VMEM)
     anywhere = pl.BlockSpec(memory_space=pl.ANY)
 
@@ -481,7 +577,7 @@
             jax.ShapeDtypeStruct(fields.shape, jnp.bfloat16),
             jax.ShapeDtypeStruct(weights.shape, jnp.bfloat16),
         ),
-        in_specs=[anywhere] * 3 + [vmem] * 6,
+        in_specs=[anywhere] * 3 + [pl.BlockSpec(memory_space=pltpu.SMEM)] + [vmem] * 7,
         out_specs=(anywhere, anywhere),
         scratch_shapes=[
             buffer(chunks, lat_dev, lons, LANES),
@@ -500,6 +596,10 @@
             pltpu.VMEM((wide_rows, LANES), jnp.float32),
             buffer(*weights.shape),
             buffer(others, *weights.shape),
+            buffer(orders, DEGREES, LATS),
+            buffer(orders, DEGREES, LATS),
+            pltpu.VMEM((DEGREES, orders, halves * LANES), jnp.float32),
+            pltpu.VMEM((halves, orders * DEGREES, LANES), jnp.float32),
             dma((2 * chunks + 1,)),
             dma((8, chunks)),
             dma((8, chunks)),
@@ -512,8 +612,7 @@
         ),
         name="filter_block",
     )(
-        fields, cotangent, weights, qtab, ptab,
-        jnp.transpose(forward), forward, inverse, jnp.transpose(inverse),
+        fields, cotangent, weights, degree_of, *floats, *waves,
     )
 
 

time: 376 us -> 364 us (0.968)
  Pallas kernels: 361 us -> 353 us
    pallas_call x1 -> x0, Pallas kernels: 4.89 us -> none  [spectral_tables(): pl.pallas_call(table_kernel, out_shape=(shape, shape), in_specs=[pl.Block...]
where the time goes in v3:
time: 364 us; the launch traced here: 360 us
  Pallas kernels  353 us (97%)
  local copies, waits for them, and re-layouts  6.5 us (2%)
    pallas_call x1, Pallas kernels, local_kernel(): pl.pallas_call(functools.partial(block_kernel, n, nb), out_shape=(jax.Sha...  353 us

profile of v3, /device:TPU:12, one launch (start us, length us, event | category | flops | bytes accessed | tf_op | source)
XLA Modules:
  0.0 360.4 jit_solution(784383547415455813)
XLA Ops:
  0.6 353.2 %filter_block.1 = (bf16[1,12,384,384]{3,2,1,0:T(8,128)(2,1)}, bf16[8,2,384,384]{3,2,1,0:T(8,128)(2,1)}) custom-call(bf16[1,12,384,384]{3,2,1,0:T(8,128)(2,1)} %fields.1, bf16[1,12,384,384]{3,2,1,0:T(8,128)(2,1)} %cotangent.1, bf16[8,2,384,384]{3,2,1,0:T(8,128)(2,1)} %weights.1, s32[128]{0:T(128)} %deg_ref.1, f32[128,256]{1,0:T(8,128)} %constant.14.clone.diag_ref, ...), custom_call_target="tpu_custom_call" | custom-call | tf_op jit(solution)/shard_map/filter_block/pallas_call | solution.py:574
  353.9 0.0 copy-start
  353.9 4.3 %copy.15 = bf16[1,12,384,384]{3,2,1,0:T(8,128)(2,1)} copy(bf16[1,12,384,384]{3,2,1,0:T(8,128)(2,1)} %get-tuple-element.4) | data formatting | bytes 7077888
  358.2 0.0 copy-done
  358.2 2.2 copy.16
Async XLA Ops:
  353.9 4.3 %copy-start = (bf16[8,2,384,384]{3,2,1,0:T(8,128)(2,1)S(1)}, bf16[8,2,384,384]{3,2,1,0:T(8,128)(2,1)}, u32[]{:S(2)}) copy-start(bf16[8,2,384,384]{3,2,1,0:T(8,128)(2,1)} %get-tuple-element.5) | copy-start | bytes 14155780
